TPU v7x, 32 devices: a whole 2x2x4 slice. The times are simulated.
32 devices in a mesh: occ: 8 (over z, core), aux: 4 (over y, x).
Axes of the slice: x: 2, y: 2, z: 4, core: 2. Of those that a mesh axis runs over, the one named last changes fastest.
Arguments:
- integrals: bfloat16 [2048, 256, 512], P('aux', 'occ'), may hold values from -1.1953125 to 1.1953125
- metric: bfloat16 [2048, 2048], replicated, may hold values from -0.125 to 0.125
- e_occ: float32 [256], replicated, may hold values from -2 to -0.3
- e_vir: float32 [512], replicated, may hold values from 0.2 to 3
- partner: int32 [256, 2], P(('occ', 'aux')), may hold values from 0 to 7
- screen: int32 [256, 2], P(('occ', 'aux')), may hold values from 0 to 1
Outputs:
- gradient: bfloat16 [2048, 256, 512], P(None, ('occ', 'aux'))
- density: float32 [512, 512], P('occ')
All inputs are finite; a program needn't handle non-finite values.
Results may differ from a plain program's by a relative error of at most 0.0055.
Values may be sent and summed in bfloat16 or wider, within the bound.
A program may use at most 192 MiB of HBM per device.

v0:
```python
import functools

import jax
import jax.numpy as jnp
from jax import lax
from jax.experimental import pallas as pl
from jax.experimental.pallas import tpu as pltpu
from jax.sharding import PartitionSpec as P

NOCC = 256
ROUNDS = 2
BOTH = ("occ", "aux")
NT = (((1,), (1,)), ((), ()))
TN = (((0,), (0,)), ((), ()))

MESH = pl.DeviceIdType.MESH


def gamma_kernel(own, at, right, amp, begun, out, rows):
    now = lax.rem(pl.program_id(0), 2)
    for i in range(own):
        term = lax.dot_general(right[at[1, i]], amp[at[3, i]], NT, preferred_element_type=jnp.float32)
        rows[now, i] = (begun[i] + term).astype(rows.dtype)
    out[...] = pltpu.einshape("ipa->pia", rows[1 - now])


def gradient(right, amp, begun, ints):
    own, naux, nvir = right.shape
    tile = min(256, naux)
    tiles = naux // tile
    this = lambda p, *_: (0, jnp.minimum(p, tiles - 1), 0)
    return pl.pallas_call(
        functools.partial(gamma_kernel, own),
        grid_spec=pltpu.PrefetchScalarGridSpec(
            num_scalar_prefetch=1,
            grid=(tiles + 1,),
            in_specs=[
                pl.BlockSpec((own, tile, nvir), this),
                pl.BlockSpec(amp.shape, lambda p, *_: (0, 0, 0)),
                pl.BlockSpec((own, tile, nvir), this),
            ],
            out_specs=pl.BlockSpec((tile, own, nvir), lambda p, *_: (jnp.maximum(p - 1, 0), 0, 0)),
            scratch_shapes=[pltpu.VMEM((2, own, tile, nvir), jnp.bfloat16)],
        ),
        out_shape=jax.ShapeDtypeStruct((naux, own, nvir), jnp.bfloat16),
    )(ints, right, amp, begun)


def table_kernel(n_occ, n_aux, row, table, send, recv, local):
    groups = n_occ * n_aux
    me = lax.axis_index("occ") * n_aux + lax.axis_index("aux")
    barrier = pltpu.get_barrier_semaphore()

    def place(step):
        other = lax.rem(me + step, groups)
        return (other // n_aux, lax.rem(other, n_aux))

    def greet(step, carry):
        pl.semaphore_signal(barrier, inc=1, device_id=place(step), device_id_type=MESH)
        return carry

    lax.fori_loop(1, groups, greet, 0)
    own = pltpu.make_async_copy(row, table.at[me], local)
    own.start()
    pl.semaphore_wait(barrier, groups - 1)

    def copy(step):
        return pltpu.make_async_remote_copy(
            row, table.at[me], send.at[step], recv.at[step], device_id=place(step), device_id_type=MESH
        )

    def start(step, carry):
        copy(step).start()
        return carry

    def finish(step, carry):
        came = lax.rem(me - step + groups, groups)
        pltpu.make_async_remote_copy(
            row, table.at[came], send.at[step], recv.at[step], device_id=place(step), device_id_type=MESH
        ).wait()
        return carry

    lax.fori_loop(1, groups, start, 0)
    own.wait()
    lax.fori_loop(1, groups, finish, 0)


def everyones(row, n_occ, n_aux):
    groups = n_occ * n_aux
    return pl.pallas_call(
        functools.partial(table_kernel, n_occ, n_aux),
        out_shape=jax.ShapeDtypeStruct((groups,) + row.shape, row.dtype),
        in_specs=[pl.BlockSpec(memory_space=pltpu.VMEM)],
        out_specs=pl.BlockSpec(memory_space=pltpu.VMEM),
        scratch_shapes=[
            pltpu.SemaphoreType.DMA((groups,)),
            pltpu.SemaphoreType.DMA((groups,)),
            pltpu.SemaphoreType.DMA(()),
        ],
        compiler_params=pltpu.CompilerParams(collective_id=0, has_side_effects=True),
    )(row)


def pack_kernel(base, table, x, out, turned):
    n_aux, own = out.shape[:2]
    turned[...] = pltpu.einshape("qja->jqa", x[...])
    for slot in range(n_aux * own):
        reader = base[0] + slot // own
        out[slot // own, slot % own] = turned[slot // own * own + table[reader, own + slot % own]]


def packed_blocks(x, base, table, n_aux):
    depth, held, nvir = x.shape
    own = held // n_aux
    tile = min(32, depth)
    return pl.pallas_call(
        pack_kernel,
        grid_spec=pltpu.PrefetchScalarGridSpec(
            num_scalar_prefetch=2,
            grid=(depth // tile,),
            in_specs=[pl.BlockSpec((tile, held, nvir), lambda q, *_: (q, 0, 0))],
            out_specs=pl.BlockSpec((n_aux, own, tile, nvir), lambda q, *_: (0, 0, q, 0)),
            scratch_shapes=[pltpu.VMEM((held, tile, nvir), x.dtype)],
        ),
        out_shape=jax.ShapeDtypeStruct((n_aux, own, depth, nvir), x.dtype),
    )(base, table, x)


def peer_of(i, step, n_aux):
    return i ^ step if n_aux & (n_aux - 1) == 0 else lax.rem(step + n_aux - i, n_aux)


def shares(total, own, core):
    caps = ((total + 1) // 2, total // 2)
    spill = tuple(min(own - caps[1 - c], caps[c]) for c in range(2))
    pick = lambda pair: pair[0] + core * (pair[1] - pair[0])
    return pick(caps), pick(caps[::-1]), pick(spill), pick(spill[::-1])


def move_kernel(
    total, n_occ, n_aux, ints, floats, packed, mixed, col, row,
    far, begun, coeff, wrapped, fills, amp, block_out,
    pool, lent, stage, term, kept_amp, parts, half, sum1, from_side, from_aux, from_z, gathered,
    sent, came, far_sent, far_came, side_sent, side_came, cross_sent, cross_came,
    wrap_sems, local, stored, fold_sent, fold_came,
):
    own, depth = packed.shape[1:3]
    naux, nvir = stage.shape
    occ, aux = lax.axis_index("occ"), lax.axis_index("aux")
    core = lax.rem(occ, 2)
    cap, cap_mate, spill, spill_mate = shares(total, own, core)
    most_z = n_occ // 2
    mate = (lax.rem(occ + n_occ // 2, n_occ), aux)
    after = (lax.rem(occ + 1, n_occ), aux)
    before = (lax.rem(occ + n_occ - 1, n_occ), aux)
    side = (occ + 1 - 2 * core, aux)
    peers = [(occ, peer_of(aux, s, n_aux)) for s in range(n_aux)]
    column = [(lax.rem(occ + 2 * k, n_occ), aux) for k in range(most_z)]
    column_before = [(lax.rem(occ + n_occ - 2 * k, n_occ), aux) for k in range(most_z)]

    barrier = pltpu.get_barrier_semaphore()
    greeted = [after, before, side] + peers[1:] + column[1:]
    for device in greeted:
        pl.semaphore_signal(barrier, inc=1, device_id=device, device_id_type=MESH)
    pl.semaphore_wait(barrier, len(greeted))

    def remote(source, target, send, recv, device):
        return pltpu.make_async_remote_copy(source, target, send, recv, device_id=device, device_id_type=MESH)

    wrap = remote(packed.at[n_aux - 1], wrapped, wrap_sems.at[0], wrap_sems.at[1], after)
    wrap.start()

    def part(land, t, q):
        return land.at[t, pl.ds(pl.multiple_of(q * depth, depth), depth)]

    def piece(kind, land, source, t, s, q):
        if s == 0:
            return pltpu.make_async_copy(source, part(land, t, q), local.at[kind, t])
        return remote(source, part(land, t, q), sent.at[kind, t, s], came.at[kind, t, s], peers[s])

    def send_own(t, carry):
        for s in range(n_aux):
            piece(0, pool, packed.at[peers[s][1], t], t, s, aux).start()
        return carry

    def send_near(t, carry):
        for s in range(n_aux):
            to = peers[s][1]

            @pl.when(to == 0)
            def _():
                piece(1, lent, wrapped.at[t], t, s, aux).start()

            @pl.when(to != 0)
            def _():
                piece(1, lent, packed.at[jnp.maximum(to - 1, 0), t], t, s, aux).start()

        return carry

    tile = min(256, naux)

    def put(source, target):
        out = pltpu.make_async_copy(source, target, stored)
        out.start()
        out.wait()

    def transform(kind, land, t):
        for s in range(n_aux):
            move = piece(kind, land, packed.at[0, 0], t, s, peers[s][1])
            move.wait() if s == 0 else move.wait_recv()

        def rows(i, carry):
            at = pl.ds(pl.multiple_of(i * tile, tile), tile)
            stage[at, :] = jnp.dot(mixed[at, :], land[t], preferred_element_type=jnp.float32).astype(stage.dtype)
            return carry

        def back(i, carry):
            at = pl.ds(pl.multiple_of(i * tile, tile), tile)
            land[t, at, :] = stage[at, :]
            return carry

        lax.fori_loop(0, naux // tile, rows, 0)
        lax.fori_loop(0, naux // tile, back, 0)

    def far_copy(source, t):
        return remote(source, far.at[t], far_sent.at[t], far_came.at[t], mate)

    def side_copy(t, x):
        return remote(coeff.at[t], pool.at[own + x], side_sent.at[x], side_came.at[x], side)

    def cross_copy(t, f, place):
        return remote(far.at[t], far.at[place + f], cross_sent.at[f], cross_came.at[f], side)

    def own_slot(t, carry):
        @pl.when(t == min(own - 1, 2))
        def _():
            wrap.wait()
            lax.fori_loop(0, own, send_near, 0)

        transform(0, pool, t)
        put(pool.at[t], coeff.at[t])

        @pl.when(t < cap - spill)
        def _():
            far_copy(coeff.at[t], t).start()

        @pl.when((t >= cap) & (t < cap + spill_mate))
        def _():
            side_copy(t, jnp.maximum(t - cap, 0)).start()

        return carry

    def near_slot(t, carry):
        transform(1, lent, t)
        return carry

    lax.fori_loop(0, own, send_own, 0)
    lax.fori_loop(0, own, own_slot, 0)

    def side_wait(x, carry):
        side_copy(0, x).wait_recv()
        return carry

    lax.fori_loop(0, spill, side_wait, 0)

    def fill(f, carry):
        def copy(i, inner):
            at = pl.ds(pl.multiple_of(i * tile, tile), tile)
            stage[at, :] = pool[ints[2, f], at, :]
            return inner

        lax.fori_loop(0, naux // tile, copy, 0)
        put(stage, fills.at[f])
        far_copy(fills.at[f], cap - spill + f).start()
        return carry

    lax.fori_loop(0, spill, fill, 0)
    lax.fori_loop(0, own, near_slot, 0)

    parts[...] = jnp.zeros_like(parts)

    def amplitude(left, right, kept, gap):
        both = lax.dot_general(left, right, TN, preferred_element_type=jnp.float32)
        block = (kept * both / (col[...] + row[...] - gap[0] - gap[1])).astype(amp.dtype)
        square = lax.dot_general(block, block, NT, preferred_element_type=jnp.float32)
        parts[...] += square.reshape(parts.shape)
        return block

    def pair0(i, carry):
        kept_amp[...] = amplitude(pool[ints[4, i]], lent[ints[0, i]], floats[0, i], (floats[2, i], floats[4, i]))

        def rows(k, inner):
            at = pl.ds(pl.multiple_of(k * tile, tile), tile)
            term[at, :] = lax.dot_general(
                lent[ints[0, i], at, :], kept_amp[...], NT, preferred_element_type=jnp.float32
            )
            return inner

        lax.fori_loop(0, naux // tile, rows, 0)
        put(term, begun.at[i])
        return carry

    lax.fori_loop(0, own, pair0, 0)

    def pair1(m):
        amp[m] = amplitude(pool[ints[5, m]], lent[ints[6, m]], floats[1, m], (floats[3, m], floats[5, m]))

    def crossed(f, carry):
        cross_copy(0, f, cap).wait_recv()
        put(far.at[cap + f], lent.at[cap + f])
        return carry

    def next_pair(m, carry):
        @pl.when(m < cap)
        def _():
            far_copy(coeff.at[m], m).wait_recv()

            @pl.when(m >= cap - spill)
            def _():
                cross_copy(m, jnp.maximum(m - (cap - spill), 0), cap_mate).start()

            put(far.at[m], lent.at[m])

        @pl.when(m == cap)
        def _():
            lax.fori_loop(0, spill_mate, crossed, 0)

        pair1(m)
        return carry

    lax.fori_loop(0, own, next_pair, 0)

    fold = lambda k, source, target, device: remote(source, target, fold_sent.at[k], fold_came.at[k], device)
    swap = fold(0, parts.at[:, 1 - core], from_side, side)
    swap.start()
    swap.wait()
    half[...] = parts[:, core] + from_side[...]
    moves = [fold(s, half.at[:, peers[s][1]], from_aux.at[s - 1], peers[s]) for s in range(1, n_aux)]
    for move in moves:
        move.start()
    for move in moves:
        move.wait()
    sum1[...] = half[:, aux] + jnp.sum(from_aux[...], axis=0)
    moves = []
    for k in range(1, most_z):
        moves.append(fold(n_aux + k - 1, sum1.at[column[k][0] // 2], from_z.at[k - 1], column[k]))
    for move in moves:
        move.start()
    for move in moves:
        move.wait()
    gathered[aux] = (sum1[occ // 2] + jnp.sum(from_z[...], axis=0)) / NOCC
    base = n_aux + most_z - 2
    moves = [fold(base + s, gathered.at[aux], gathered.at[aux], peers[s]) for s in range(1, n_aux)]
    for move in moves:
        move.start()
    for s, move in enumerate(moves):
        move.wait_send()
        fold(base + s + 1, gathered.at[aux], gathered.at[peers[s + 1][1]], peers[s + 1]).wait_recv()
    block_out[...] = gathered[...].reshape(block_out.shape)

    def drain(t, carry):
        for kind, land in ((0, pool), (1, lent)):
            for s in range(1, n_aux):
                piece(kind, land, packed.at[0, 0], t, s, aux).wait_send()
        return carry

    def side_drain(x, carry):
        side_copy(0, x).wait_send()
        return carry

    def far_drain(t, carry):
        far_copy(coeff.at[t], t).wait_send()
        return carry

    def cross_drain(f, carry):
        cross_copy(0, f, cap_mate).wait_send()
        return carry

    lax.fori_loop(0, own, drain, 0)
    lax.fori_loop(0, spill_mate, side_drain, 0)
    lax.fori_loop(0, cap, far_drain, 0)
    lax.fori_loop(0, spill, cross_drain, 0)


def moved(packed, mixed, e_vir, ints, floats, total, n_occ, n_aux):
    _, own, depth, nvir = packed.shape
    naux = depth * n_aux
    spill = max(1, *(shares(total, own, core)[2] for core in range(2)))
    anywhere = pl.BlockSpec(memory_space=pl.ANY)
    fast = pl.BlockSpec(memory_space=pltpu.VMEM)
    scalars = pl.BlockSpec(memory_space=pltpu.SMEM)
    kind = packed.dtype
    dma = pltpu.SemaphoreType.DMA
    wide = lambda count: jax.ShapeDtypeStruct((count, naux, nvir), kind)
    most_z, thin = n_occ // 2, nvir // (n_occ * n_aux)
    single = lambda *lead: pltpu.VMEM(lead + (thin, nvir), jnp.float32)
    folds = 2 * n_aux + most_z - 1
    return pl.pallas_call(
        functools.partial(move_kernel, total, n_occ, n_aux),
        out_shape=[
            wide(own),
            jax.ShapeDtypeStruct((own, naux, nvir), jnp.float32),
            wide(own),
            jax.ShapeDtypeStruct((own, depth, nvir), kind),
            wide(spill),
            jax.ShapeDtypeStruct((own, nvir, nvir), kind),
            jax.ShapeDtypeStruct((nvir // n_occ, nvir), jnp.float32),
        ],
        in_specs=[scalars] * 2 + [anywhere, fast, fast, fast],
        out_specs=[anywhere] * 5 + [fast] * 2,
        scratch_shapes=[
            pltpu.VMEM((own + spill, naux, nvir), kind),
            pltpu.VMEM((own, naux, nvir), kind),
            pltpu.VMEM((naux, nvir), kind),
            pltpu.VMEM((naux, nvir), jnp.float32),
            pltpu.VMEM((nvir, nvir), kind),
            single(most_z, 2, n_aux),
            single(most_z, n_aux),
            single(most_z),
            single(most_z, n_aux),
            single(n_aux - 1, most_z),
            single(most_z - 1),
            single(n_aux),
            dma((2, own, n_aux)),
            dma((2, own, n_aux)),
            dma((own,)),
            dma((own,)),
            dma((spill,)),
            dma((spill,)),
            dma((spill,)),
            dma((spill,)),
            dma((2,)),
            dma((2, own)),
            dma(()),
            dma((folds,)),
            dma((folds,)),
        ],
        compiler_params=pltpu.CompilerParams(
            collective_id=total, has_side_effects=True, vmem_limit_bytes=67043328
        ),
    )(ints, floats, packed, mixed, e_vir[:, None], e_vir[None, :])


def plan_kernel(choices, n_occ, n_aux, table, partner, screen, e_occ, ints, floats, branch):
    groups = n_occ * n_aux
    own = partner.shape[0]
    occ, aux = lax.axis_index("occ"), lax.axis_index("aux")
    device = occ * n_aux + aux
    far_by = groups // 2
    reader = lambda source: lax.rem(source + far_by, groups)
    count = lambda source: table[reader(source), 2 * own]

    def chip(c, most):
        source = c // n_aux * 2 * n_aux + lax.rem(c, n_aux)
        return jnp.maximum(most, count(source) + count(source + n_aux))

    most = lax.fori_loop(0, groups // 2, chip, 0)
    chosen, total = 0, choices[0]
    for k in range(1, len(choices)):
        over = most > choices[k - 1]
        chosen = jnp.where(over, k, chosen)
        total = jnp.where(over, choices[k], total)
    branch[0] = jnp.int32(chosen)
    core = lax.rem(occ, 2)
    caps = ((total + 1) // 2, total // 2)
    cap, cap_mate = jnp.where(core == 0, caps[0], caps[1]), jnp.where(core == 0, caps[1], caps[0])
    spill, spill_mate = jnp.minimum(own - cap_mate, cap), jnp.minimum(own - cap, cap_mate)
    side_count = count((occ + 1 - 2 * core) * n_aux + aux)
    near, far = lax.rem(device + groups - 1, groups), lax.rem(device + groups - far_by, groups)
    ranks = [table[reader(far), partner[i, 1]] for i in range(own)]
    keys = [jnp.where(screen[i, 1] != 0, ranks[i], own) for i in range(own)]
    for i in range(own):
        ints[0, i] = table[reader(near), partner[i, 0]]
        beyond = cap + spill_mate - 1 - (ranks[i] - cap)
        slot = jnp.clip(jnp.where(ranks[i] < cap, ranks[i], beyond), 0, own - 1)
        ints[1, i] = slot
        step = spill - 1 - i
        fill = jnp.where(step < side_count - cap_mate, own + step, cap - spill + i)
        ints[2, i] = jnp.clip(fill, 0, own - 1 + jnp.maximum(spill, 1))
        where = jnp.int32(0)
        for other in range(own):
            if other != i:
                ahead = keys[other] < keys[i] if other > i else keys[other] <= keys[i]
                where = where + jnp.where(ahead, 1, 0)
        ints[3, i] = where
        mine = table[reader(device), i]
        ints[4, i] = mine
        ints[5, where] = mine
        ints[6, where] = slot
        floats[0, i] = screen[i, 0].astype(jnp.float32)
        floats[1, where] = screen[i, 1].astype(jnp.float32)
        energy = e_occ[device * own + i]
        floats[2, i] = energy
        floats[3, where] = energy
        floats[4, i] = e_occ[near * own + partner[i, 0]]
        floats[5, where] = e_occ[far * own + partner[i, 1]]


def plan(choices, table, partner, screen, e_occ, n_occ, n_aux):
    own = partner.shape[0]
    scalars = pl.BlockSpec(memory_space=pltpu.SMEM)
    return pl.pallas_call(
        functools.partial(plan_kernel, choices, n_occ, n_aux),
        out_shape=[
            jax.ShapeDtypeStruct((7, own), jnp.int32),
            jax.ShapeDtypeStruct((6, own), jnp.float32),
            jax.ShapeDtypeStruct((1,), jnp.int32),
        ],
        in_specs=[scalars] * 4,
        out_specs=[scalars] * 3,
    )(table, partner, screen, e_occ)


def on_device(integrals, metric, e_occ, e_vir, partner, screen):
    n_occ, n_aux = lax.axis_size("occ"), lax.axis_size("aux")
    groups = n_occ * n_aux
    depth, held, nvir = integrals.shape
    own = held // n_aux
    naux = depth * n_aux
    occ, aux = lax.axis_index("occ"), lax.axis_index("aux")
    device = occ * n_aux + aux

    place = jnp.arange(own, dtype=jnp.int32)
    wanted = jnp.any((partner[:, 1, None] == place) & (screen[:, 1, None] != 0), axis=0)
    below = place[None, :] < place[:, None]
    count = jnp.sum(wanted, dtype=jnp.int32)
    first = jnp.sum(below & wanted[None, :], axis=1, dtype=jnp.int32)
    rank = jnp.where(wanted, first, count + place - first)
    order = jnp.sum(jnp.where(rank[None, :] == place[:, None], place[None, :], 0), axis=1)
    lines = jnp.concatenate([rank, order, count[None]])[None]
    lines = jnp.pad(lines, ((0, 7), (0, 128 - 2 * own - 1)))
    table = everyones(lines, n_occ, n_aux)[:, 0, :]

    reader = ((occ + n_occ // 2) % n_occ) * n_aux
    packed = packed_blocks(integrals, reader[None], table, n_aux)

    choices = sorted(set(range(own + 2, 2 * own - 2)) | {2 * own})
    ints, floats, branch = plan(choices, table, partner, screen, e_occ, n_occ, n_aux)

    def chosen(total):
        far, begun, _, _, _, amp, block = moved(packed, metric, e_vir, ints, floats, total, n_occ, n_aux)
        return far, begun, amp, block

    far, begun, amp, block = lax.switch(branch[0], [functools.partial(chosen, total) for total in choices])
    return gradient(far, amp, begun, ints), block


def solution(mesh):
    return jax.shard_map(
        on_device,
        mesh=mesh,
        in_specs=(P("aux", "occ", None), P(), P(), P(), P(BOTH, None), P(BOTH, None)),
        out_specs=(P(None, BOTH, None), P("occ", None)),
        check_vma=False,
    )
```

profile of v0, /device:TPU:0, one launch (start us, length us, event | category | flops | bytes accessed | tf_op | source)
XLA Modules:
  0.0 699.8 jit_solution(16038133418209384711)
XLA Ops:
  0.6 0.7 slice_bitcast_fusion
  1.3 0.7 compare_bitcast_fusion
  2.0 0.1 fusion.1
  2.1 0.6 convert_reduce_fusion.1
  2.7 0.1 convert_reduce_fusion
  2.9 0.7 subtract_select_fusion
  3.5 0.1 select_reduce_fusion
  3.6 0.7 add_bitcast_fusion
  4.3 0.6 pad.4.row
  5.0 1.3 copy.25.partner
  6.3 1.3 copy.26.screen
  7.6 11.8 %shard_map.77 = s32[32,8,128]{2,1,0:T(8,128)} custom-call(s32[8,128]{1,0:T(8,128)} %pad.4.row), custom_call_target="tpu_custom_call" | custom-call | tf_op jit(solution)/shard_map/pallas_call | solution.py:90
  19.5 1.5 slice.11
  21.0 2.3 shard_map.78
  23.9 0.0 copy-start
  23.9 20.6 %shard_map.79 = bf16[4,8,512,512]{3,2,1,0:T(8,128)(2,1)} custom-call(s32[1]{0:T(128)} %bitcast.16.base, s32[32,128]{1,0:T(8,128)} %bitcast.33, bf16[512,32,512]{2,1,0:T(8,128)(2,1)} %x.3), custom_call_target="tpu_custom_call" | custom-call | tf_op jit(solution)/shard_map/pallas_call | solution.py:116
  44.5 0.0 copy-done
  44.6 626.8 %conditional.1 = (bf16[8,2048,512]{2,1,0:T(8,128)(2,1)}, f32[8,2048,512]{2,1,0:T(8,128)}, bf16[8,512,512]{2,1,0:T(8,128)(2,1)}, f32[64,512]{1,0:T(8,128)}) conditional(s32[]{:T(128)} %bitcast.15, (f32[512]{0:T(512)S(1)}, s32[7,8]{1,0:T(8,128)}, f32[6,8]{1,0:T(8,128)}, bf16[4,8,512,512]{3,2,1,0:T(8,128)(2,1)}, ...), branch_computations={%region_4.5_spmd, %region_5.6_spmd, %region_6.7_spmd, %region_7.8_... | conditional | bytes 12348 | solution.py:544
  44.6 0.6 copy-done.3
  45.1 0.9 copy.21.col
  46.0 625.2 %branch_2_fun.1 = (bf16[8,2048,512]{2,1,0:T(8,128)(2,1)}, f32[8,2048,512]{2,1,0:T(8,128)}, bf16[8,2048,512]{2,1,0:T(8,128)(2,1)}, bf16[8,512,512]{2,1,0:T(8,128)...) custom-call(s32[7,8]{1,0:T(8,128)} %get-tuple-element.68.ints, ...), custom_call_target="tpu_custom_call" | custom-call | tf_op jit(solution)/shard_map/cond/branch_2_fun/pallas_call | solution.py:398
  671.4 0.0 copy-start.6
  671.4 27.8 %shard_map.80 = bf16[2048,8,512]{2,1,0:T(8,128)(2,1)} custom-call(s32[7,8]{1,0:T(8,128)} %get-tuple-element.104.at, bf16[8,2048,512]{2,1,0:T(8,128)(2,1)} %get-tuple-element.107.right, bf16[8,512,512]{2,1,0:T(8,128)(2,1)} %get-tuple-element.108.amp, f32[8,2048,512]{2,1,0:T(8,128)} %get-tuple-element.109.begun), custom_call_target="tpu_custom_call" | custom-call | tf_op jit(solution)/shard_map/pallas_call | solution.py:32
  699.2 0.7 copy.49
  (2 shorter events, 0.0 us)
Async XLA Ops:
  23.9 20.6 %copy-start = (f32[512]{0:T(512)S(1)}, f32[512]{0:T(512)}, u32[]{:S(2)}) copy-start(f32[512]{0:T(512)} %param.14) | copy-start | bytes 6148
  44.6 0.6 copy-start.3
  671.4 27.8 %copy-start.6 = (f32[64,512]{1,0:T(8,128)S(1)}, f32[64,512]{1,0:T(8,128)}, u32[]{:S(2)}) copy-start(f32[64,512]{1,0:T(8,128)} %get-tuple-element.134) | copy-start | bytes 393220
where the time goes:
time: 701 us; the launch traced here: 700 us
  Pallas kernels  688 us (98%)
  local copies, waits for them, and re-layouts  7.6 us (1%)
    pallas_call x1, Pallas kernels, moved(): pl.pallas_call(functools.partial(move_kernel, total, n_occ, n_aux), out_s...  625 us
    pallas_call x1, Pallas kernels, gradient(): pl.pallas_call(functools.partial(gamma_kernel, own), grid_spec=pltpu.Pref...  27.8 us
    pallas_call x1, Pallas kernels, packed_blocks(): pl.pallas_call(pack_kernel, grid_spec=pltpu.PrefetchScalarGridSpec(num_sc...  20.6 us

commit v1 on v0

--- a/solution.py
+++ b/solution.py
@@ -25,7 +25,8 @@
 
 
 def gradient(right, amp, begun, ints):
-    own, naux, nvir = right.shape
+    slots, naux, nvir = right.shape
+    own = amp.shape[0]
     tile = min(256, naux)
     tiles = naux // tile
     this = lambda p, *_: (0, jnp.minimum(p, tiles - 1), 0)
@@ -35,7 +36,7 @@
             num_scalar_prefetch=1,
             grid=(tiles + 1,),
             in_specs=[
-                pl.BlockSpec((own, tile, nvir), this),
+                pl.BlockSpec((slots, tile, nvir), this),
                 pl.BlockSpec(amp.shape, lambda p, *_: (0, 0, 0)),
                 pl.BlockSpec((own, tile, nvir), this),
             ],
@@ -46,9 +47,34 @@
     )(ints, right, amp, begun)
 
 
-def table_kernel(n_occ, n_aux, row, table, send, recv, local):
+def table_kernel(n_occ, n_aux, partner, screen, table, row, send, recv, local):
     groups = n_occ * n_aux
+    own = partner.shape[0]
     me = lax.axis_index("occ") * n_aux + lax.axis_index("aux")
+
+    def wants(k):
+        found = jnp.int32(0)
+        for i in range(own):
+            found = jnp.where((partner[i, 1] == k) & (screen[i, 1] != 0), 1, found)
+        return found
+
+    wanted = [wants(k) for k in range(own)]
+    total = sum(wanted)
+    lend = (total >= own // 2 + 1) & (total < own)
+    ahead, slots = jnp.int32(0), []
+    for k in range(own):
+        behind = jnp.where(lend, total - 1, total) + k - ahead
+        last = jnp.where(lend & (ahead == total - 1), own - 1, ahead)
+        slots.append(jnp.where(wanted[k] == 1, last, behind))
+        ahead = ahead + wanted[k]
+    lane = lax.broadcasted_iota(jnp.int32, (1, 128), 1)
+    line = jnp.where(lane == 2 * own, total, 0)
+    for k in range(own):
+        line = line + jnp.where(lane == k, slots[k], 0)
+        turned = sum(jnp.where(slots[j] == k, j, 0) for j in range(own))
+        line = line + jnp.where(lane == own + k, turned, 0)
+    row[...] = line
+
     barrier = pltpu.get_barrier_semaphore()
 
     def place(step):
@@ -60,45 +86,44 @@
         return carry
 
     lax.fori_loop(1, groups, greet, 0)
-    own = pltpu.make_async_copy(row, table.at[me], local)
-    own.start()
+    own_row = pltpu.make_async_copy(row, table.at[me], local)
+    own_row.start()
     pl.semaphore_wait(barrier, groups - 1)
 
-    def copy(step):
+    def copy(step, came):
         return pltpu.make_async_remote_copy(
-            row, table.at[me], send.at[step], recv.at[step], device_id=place(step), device_id_type=MESH
+            row, table.at[came], send.at[step], recv.at[step], device_id=place(step), device_id_type=MESH
         )
 
     def start(step, carry):
-        copy(step).start()
+        copy(step, me).start()
         return carry
 
     def finish(step, carry):
-        came = lax.rem(me - step + groups, groups)
-        pltpu.make_async_remote_copy(
-            row, table.at[came], send.at[step], recv.at[step], device_id=place(step), device_id_type=MESH
-        ).wait()
+        copy(step, lax.rem(me - step + groups, groups)).wait()
         return carry
 
     lax.fori_loop(1, groups, start, 0)
-    own.wait()
+    own_row.wait()
     lax.fori_loop(1, groups, finish, 0)
 
 
-def everyones(row, n_occ, n_aux):
+def rankings(partner, screen, n_occ, n_aux):
     groups = n_occ * n_aux
+    scalars = pl.BlockSpec(memory_space=pltpu.SMEM)
     return pl.pallas_call(
         functools.partial(table_kernel, n_occ, n_aux),
-        out_shape=jax.ShapeDtypeStruct((groups,) + row.shape, row.dtype),
-        in_specs=[pl.BlockSpec(memory_space=pltpu.VMEM)],
+        out_shape=jax.ShapeDtypeStruct((groups, 1, 128), jnp.int32),
+        in_specs=[scalars] * 2,
         out_specs=pl.BlockSpec(memory_space=pltpu.VMEM),
         scratch_shapes=[
+            pltpu.VMEM((1, 128), jnp.int32),
             pltpu.SemaphoreType.DMA((groups,)),
             pltpu.SemaphoreType.DMA((groups,)),
             pltpu.SemaphoreType.DMA(()),
         ],
         compiler_params=pltpu.CompilerParams(collective_id=0, has_side_effects=True),
-    )(row)
+    )(partner, screen)
 
 
 def pack_kernel(base, table, x, out, turned):
@@ -106,7 +131,7 @@
     turned[...] = pltpu.einshape("qja->jqa", x[...])
     for slot in range(n_aux * own):
         reader = base[0] + slot // own
-        out[slot // own, slot % own] = turned[slot // own * own + table[reader, own + slot % own]]
+        out[slot // own, slot % own] = turned[slot // own * own + table[reader, 0, own + slot % own]]
 
 
 def packed_blocks(x, base, table, n_aux):
@@ -130,11 +155,15 @@
     return i ^ step if n_aux & (n_aux - 1) == 0 else lax.rem(step + n_aux - i, n_aux)
 
 
-def shares(total, own, core):
+def shares(total, own):
     caps = ((total + 1) // 2, total // 2)
-    spill = tuple(min(own - caps[1 - c], caps[c]) for c in range(2))
-    pick = lambda pair: pair[0] + core * (pair[1] - pair[0])
-    return pick(caps), pick(caps[::-1]), pick(spill), pick(spill[::-1])
+    spill = tuple(jnp.minimum(own - caps[1 - c], caps[c]) for c in range(2))
+    return caps, spill
+
+
+def fixed_shares(total, own):
+    caps = ((total + 1) // 2, total // 2)
+    return caps, tuple(min(own - caps[1 - c], caps[c]) for c in range(2))
 
 
 def move_kernel(
@@ -142,18 +171,23 @@
     far, begun, coeff, wrapped, fills, amp, block_out,
     pool, lent, stage, term, kept_amp, parts, half, sum1, from_side, from_aux, from_z, gathered,
     sent, came, far_sent, far_came, side_sent, side_came, cross_sent, cross_came,
-    wrap_sems, local, stored, fold_sent, fold_came,
+    wrap_sems, local, stored, fold_sent, fold_came, lend_sent, lend_came,
 ):
     own, depth = packed.shape[1:3]
     naux, nvir = stage.shape
     occ, aux = lax.axis_index("occ"), lax.axis_index("aux")
     core = lax.rem(occ, 2)
-    cap, cap_mate, spill, spill_mate = shares(total, own, core)
+    pick = lambda pair: pair[0] + core * (pair[1] - pair[0])
+    caps, spills = fixed_shares(total, own)
+    cap, cap_mate, spill, spill_mate = pick(caps), pick(caps[::-1]), pick(spills), pick(spills[::-1])
+    pooled = total < 2 * own
+    aside = own - min(caps) + 1 if pooled else 0
     most_z = n_occ // 2
     mate = (lax.rem(occ + n_occ // 2, n_occ), aux)
     after = (lax.rem(occ + 1, n_occ), aux)
     before = (lax.rem(occ + n_occ - 1, n_occ), aux)
     side = (occ + 1 - 2 * core, aux)
+    above = (occ + 2 - 4 * lax.rem(occ // 2, 2), aux)
     peers = [(occ, peer_of(aux, s, n_aux)) for s in range(n_aux)]
     column = [(lax.rem(occ + 2 * k, n_occ), aux) for k in range(most_z)]
     column_before = [(lax.rem(occ + n_occ - 2 * k, n_occ), aux) for k in range(most_z)]
@@ -178,7 +212,8 @@
             return pltpu.make_async_copy(source, part(land, t, q), local.at[kind, t])
         return remote(source, part(land, t, q), sent.at[kind, t, s], came.at[kind, t, s], peers[s])
 
-    def send_own(t, carry):
+    def send_own(step, carry):
+        t = lax.rem(step + own - 1, own) if pooled else step
         for s in range(n_aux):
             piece(0, pool, packed.at[peers[s][1], t], t, s, aux).start()
         return carry
@@ -231,8 +266,16 @@
     def cross_copy(t, f, place):
         return remote(far.at[t], far.at[place + f], cross_sent.at[f], cross_came.at[f], side)
 
-    def own_slot(t, carry):
-        @pl.when(t == min(own - 1, 2))
+    def lend_copy():
+        return remote(coeff.at[own - 1], pool.at[own + aside], lend_sent.at[0], lend_came.at[0], above)
+
+    def back_copy():
+        return remote(far.at[cap - spill], far.at[own], lend_sent.at[1], lend_came.at[1], above)
+
+    def own_slot(step, carry):
+        t = lax.rem(step + own - 1, own) if pooled else step
+
+        @pl.when(step == min(own - 1, 2))
         def _():
             wrap.wait()
             lax.fori_loop(0, own, send_near, 0)
@@ -244,9 +287,15 @@
         def _():
             far_copy(coeff.at[t], t).start()
 
-        @pl.when((t >= cap) & (t < cap + spill_mate))
-        def _():
-            side_copy(t, jnp.maximum(t - cap, 0)).start()
+        if pooled:
+
+            @pl.when(t >= cap - 1)
+            def _():
+                side_copy(t, jnp.maximum(t - (cap - 1), 0)).start()
+
+            @pl.when(t == own - 1)
+            def _():
+                lend_copy().start()
 
         return carry
 
@@ -261,7 +310,9 @@
         side_copy(0, x).wait_recv()
         return carry
 
-    lax.fori_loop(0, spill, side_wait, 0)
+    if pooled:
+        lax.fori_loop(0, own - cap_mate + 1, side_wait, 0)
+        lend_copy().wait_recv()
 
     def fill(f, carry):
         def copy(i, inner):
@@ -291,44 +342,54 @@
 
         def rows(k, inner):
             at = pl.ds(pl.multiple_of(k * tile, tile), tile)
-            term[at, :] = lax.dot_general(
+            term[...] = lax.dot_general(
                 lent[ints[0, i], at, :], kept_amp[...], NT, preferred_element_type=jnp.float32
             )
+            put(term, begun.at[i, at])
             return inner
 
         lax.fori_loop(0, naux // tile, rows, 0)
-        put(term, begun.at[i])
         return carry
 
     lax.fori_loop(0, own, pair0, 0)
 
-    def pair1(m):
-        amp[m] = amplitude(pool[ints[5, m]], lent[ints[6, m]], floats[1, m], (floats[3, m], floats[5, m]))
+    def pair1(m, carry):
+        kept_amp[...] = amplitude(pool[ints[5, m]], lent[ints[6, m]], floats[1, m], (floats[3, m], floats[5, m]))
+        put(kept_amp, amp.at[m])
+        return carry
+
+    def arrive(u, carry):
+        far_copy(coeff.at[u], u).wait_recv()
+        if pooled:
+
+            @pl.when(u == cap - spill)
+            def _():
+                back_copy().start()
+
+            @pl.when(u >= cap - spill)
+            def _():
+                cross_copy(u, jnp.maximum(u - (cap - spill), 0), cap_mate).start()
+
+        put(far.at[u], lent.at[u])
+        if pooled:
+
+            @pl.when(u >= 1)
+            def _():
+                pair1(jnp.maximum(u - 1, 0), 0)
+
+        return carry
 
     def crossed(f, carry):
         cross_copy(0, f, cap).wait_recv()
         put(far.at[cap + f], lent.at[cap + f])
         return carry
 
-    def next_pair(m, carry):
-        @pl.when(m < cap)
-        def _():
-            far_copy(coeff.at[m], m).wait_recv()
-
-            @pl.when(m >= cap - spill)
-            def _():
-                cross_copy(m, jnp.maximum(m - (cap - spill), 0), cap_mate).start()
-
-            put(far.at[m], lent.at[m])
-
-        @pl.when(m == cap)
-        def _():
-            lax.fori_loop(0, spill_mate, crossed, 0)
-
-        pair1(m)
-        return carry
-
-    lax.fori_loop(0, own, next_pair, 0)
+    lax.fori_loop(0, cap, arrive, 0)
+    if pooled:
+        back_copy().wait_recv()
+        put(far.at[own], lent.at[own])
+        lax.fori_loop(0, spill_mate, crossed, 0)
+    lax.fori_loop(cap - 1 if pooled else 0, own, pair1, 0)
 
     fold = lambda k, source, target, device: remote(source, target, fold_sent.at[k], fold_came.at[k], device)
     swap = fold(0, parts.at[:, 1 - core], from_side, side)
@@ -377,15 +438,19 @@
         return carry
 
     lax.fori_loop(0, own, drain, 0)
-    lax.fori_loop(0, spill_mate, side_drain, 0)
     lax.fori_loop(0, cap, far_drain, 0)
-    lax.fori_loop(0, spill, cross_drain, 0)
+    if pooled:
+        lax.fori_loop(0, own - cap + 1, side_drain, 0)
+        lax.fori_loop(0, spill, cross_drain, 0)
+        lend_copy().wait_send()
+        back_copy().wait_send()
 
 
 def moved(packed, mixed, e_vir, ints, floats, total, n_occ, n_aux):
     _, own, depth, nvir = packed.shape
     naux = depth * n_aux
-    spill = max(1, *(shares(total, own, core)[2] for core in range(2)))
+    caps, spills = fixed_shares(total, own)
+    spill, aside = max(1, *spills), own - min(caps) + 1 if total < 2 * own else 0
     anywhere = pl.BlockSpec(memory_space=pl.ANY)
     fast = pl.BlockSpec(memory_space=pltpu.VMEM)
     scalars = pl.BlockSpec(memory_space=pltpu.SMEM)
@@ -398,7 +463,7 @@
     return pl.pallas_call(
         functools.partial(move_kernel, total, n_occ, n_aux),
         out_shape=[
-            wide(own),
+            wide(own + 1),
             jax.ShapeDtypeStruct((own, naux, nvir), jnp.float32),
             wide(own),
             jax.ShapeDtypeStruct((own, depth, nvir), kind),
@@ -407,12 +472,12 @@
             jax.ShapeDtypeStruct((nvir // n_occ, nvir), jnp.float32),
         ],
         in_specs=[scalars] * 2 + [anywhere, fast, fast, fast],
-        out_specs=[anywhere] * 5 + [fast] * 2,
+        out_specs=[anywhere] * 6 + [fast],
         scratch_shapes=[
-            pltpu.VMEM((own + spill, naux, nvir), kind),
-            pltpu.VMEM((own, naux, nvir), kind),
+            pltpu.VMEM((own + aside + 1, naux, nvir), kind),
+            pltpu.VMEM((own + 1, naux, nvir), kind),
             pltpu.VMEM((naux, nvir), kind),
-            pltpu.VMEM((naux, nvir), jnp.float32),
+            pltpu.VMEM((min(256, naux), nvir), jnp.float32),
             pltpu.VMEM((nvir, nvir), kind),
             single(most_z, 2, n_aux),
             single(most_z, n_aux),
@@ -425,8 +490,8 @@
             dma((2, own, n_aux)),
             dma((own,)),
             dma((own,)),
-            dma((spill,)),
-            dma((spill,)),
+            dma((max(1, aside),)),
+            dma((max(1, aside),)),
             dma((spill,)),
             dma((spill,)),
             dma((2,)),
@@ -434,11 +499,37 @@
             dma(()),
             dma((folds,)),
             dma((folds,)),
+            dma((2,)),
+            dma((2,)),
         ],
         compiler_params=pltpu.CompilerParams(
             collective_id=total, has_side_effects=True, vmem_limit_bytes=67043328
         ),
     )(ints, floats, packed, mixed, e_vir[:, None], e_vir[None, :])
+
+
+def lending(total, own, wanted):
+    caps, spill = shares(total, own)
+    over = [wanted[z][0] + wanted[z][1] - total for z in range(2)]
+    flag = lambda test: jnp.where(test, 1, 0)
+    lends = []
+    for z in range(2):
+        big = [wanted[z][c] > caps[c] for c in range(2)]
+        one, two = over[z] == 1, over[z] == 2
+        lends.append([flag((one & big[0]) | two), flag((one & jnp.logical_not(big[0])) | two)])
+    fine, items, excess = True, [], []
+    for z in range(2):
+        fine = fine & (over[z] <= 2)
+        for c in range(2):
+            fine = fine & ((lends[z][c] == 0) | (wanted[z][c] > caps[c]))
+        items.append(
+            [lends[1 - z][c] + jnp.maximum(wanted[z][c] - caps[c] + spill[c], 0) - lends[z][c] for c in range(2)]
+        )
+        excess.append([jnp.maximum(items[z][c] - spill[c], 0) for c in range(2)])
+        for c in range(2):
+            fine = fine & (jnp.minimum(items[z][c], spill[c]) + excess[z][1 - c] <= spill[c])
+            fine = fine & ((lends[z][0] + lends[z][1] == 0) | (lends[1 - z][c] == 0))
+    return lends, items, excess, fine
 
 
 def plan_kernel(choices, n_occ, n_aux, table, partner, screen, e_occ, ints, floats, branch):
@@ -448,45 +539,88 @@
     device = occ * n_aux + aux
     far_by = groups // 2
     reader = lambda source: lax.rem(source + far_by, groups)
-    count = lambda source: table[reader(source), 2 * own]
-
-    def chip(c, most):
-        source = c // n_aux * 2 * n_aux + lax.rem(c, n_aux)
-        return jnp.maximum(most, count(source) + count(source + n_aux))
-
-    most = lax.fori_loop(0, groups // 2, chip, 0)
-    chosen, total = 0, choices[0]
+    slot_of = lambda source, orbital: table[reader(source), 0, orbital]
+
+    def counts(first):
+        count = lambda o: table[reader(o * n_aux + aux_of), 0, 2 * own]
+        aux_of = lax.rem(first, n_aux)
+        row = first // n_aux
+        return [[count(row + 2 * z + c) for c in range(2)] for z in range(2)]
+
+    chosen, total = jnp.int32(0), jnp.int32(choices[0])
     for k in range(1, len(choices)):
-        over = most > choices[k - 1]
-        chosen = jnp.where(over, k, chosen)
-        total = jnp.where(over, choices[k], total)
-    branch[0] = jnp.int32(chosen)
+
+        def quad(q, good):
+            first = q // n_aux * 4 * n_aux + lax.rem(q, n_aux)
+            return good & jnp.where(lending(choices[k - 1], own, counts(first))[3], 1, 0)
+
+        over = lax.fori_loop(0, groups // 4, quad, jnp.int32(1)) == 0
+        still = over & (chosen == k - 1)
+        chosen = jnp.where(still, k, chosen)
+        total = jnp.where(still, choices[k], total)
+    branch[0] = chosen
+    pooled = total < 2 * own
+    caps, spills = shares(total, own)
     core = lax.rem(occ, 2)
-    caps = ((total + 1) // 2, total // 2)
-    cap, cap_mate = jnp.where(core == 0, caps[0], caps[1]), jnp.where(core == 0, caps[1], caps[0])
-    spill, spill_mate = jnp.minimum(own - cap_mate, cap), jnp.minimum(own - cap, cap_mate)
-    side_count = count((occ + 1 - 2 * core) * n_aux + aux)
+    level = lax.rem(occ // 2, 2)
+    by_core = lambda pair, c: jnp.where(c == 0, pair[0], pair[1])
+    at = lambda grid, z, c: by_core([by_core(grid[0], c), by_core(grid[1], c)], z)
+    cap, cap_mate = by_core(caps, core), by_core(caps, 1 - core)
+    spill, spill_mate = by_core(spills, core), by_core(spills, 1 - core)
+    aside = own - caps[1] + 1
+    many = own // 2 + 1
+
+    def shared_slot(item, first_shared, wanted):
+        lent = (wanted >= many) & (item == wanted - 1 - first_shared)
+        return jnp.where(lent, own - 1, first_shared + item)
+
+    wanted = counts((occ - 2 * level - core) * n_aux + aux)
+    lends, items, excess, _ = lending(total, own, wanted)
+    carries, mine, theirs = at(lends, 1 - level, core), at(items, level, core), at(excess, level, 1 - core)
+    wanted_own, wanted_side = at(wanted, level, core), at(wanted, level, 1 - core)
+    side_carries = at(lends, 1 - level, 1 - core)
+    for f in range(own):
+        own_item = shared_slot(f - carries, cap - spill, wanted_own)
+        k = f - mine
+        side_slot = shared_slot(spill_mate - side_carries + k, cap_mate - spill_mate, wanted_side)
+        side_item = jnp.where(k < theirs, own + side_slot - (cap_mate - 1), 0)
+        item = jnp.where(f < mine, own_item, side_item)
+        item = jnp.where((f == 0) & (carries == 1), own + aside, item)
+        ints[2, f] = jnp.where(pooled, jnp.clip(item, 0, own + aside), 0)
+
     near, far = lax.rem(device + groups - 1, groups), lax.rem(device + groups - far_by, groups)
-    ranks = [table[reader(far), partner[i, 1]] for i in range(own)]
-    keys = [jnp.where(screen[i, 1] != 0, ranks[i], own) for i in range(own)]
+    source_occ = far // n_aux
+    wanted = counts((source_occ - 2 * level - core) * n_aux + aux)
+    lends, items, _, _ = lending(total, own, wanted)
+    lent_one, carries = at(lends, level, core), at(lends, 1 - level, core)
+    wanted_own = at(wanted, level, core)
+    side_items = jnp.minimum(at(items, level, 1 - core), spill_mate)
+
+    def far_slot(slot):
+        special = (slot == own - 1) & (wanted_own >= many)
+        item = jnp.where(special, wanted_own - 1 - (cap - spill), slot - (cap - spill))
+        f = carries + item
+        shared = jnp.where(f < spill, cap - spill + f, cap + side_items + f - spill)
+        place = jnp.where(special & (lent_one == 1), own, shared)
+        place = jnp.where(slot < cap - spill, slot, place)
+        return jnp.clip(place, 0, own)
+
+    found = [far_slot(slot_of(far, partner[i, 1])) for i in range(own)]
+    found = [jnp.where(screen[i, 1] != 0, found[i], 0) for i in range(own)]
+    keys = [jnp.where(screen[i, 1] != 0, found[i], own + 1) for i in range(own)]
     for i in range(own):
-        ints[0, i] = table[reader(near), partner[i, 0]]
-        beyond = cap + spill_mate - 1 - (ranks[i] - cap)
-        slot = jnp.clip(jnp.where(ranks[i] < cap, ranks[i], beyond), 0, own - 1)
-        ints[1, i] = slot
-        step = spill - 1 - i
-        fill = jnp.where(step < side_count - cap_mate, own + step, cap - spill + i)
-        ints[2, i] = jnp.clip(fill, 0, own - 1 + jnp.maximum(spill, 1))
+        ints[0, i] = slot_of(near, partner[i, 0])
+        ints[1, i] = found[i]
         where = jnp.int32(0)
         for other in range(own):
             if other != i:
                 ahead = keys[other] < keys[i] if other > i else keys[other] <= keys[i]
                 where = where + jnp.where(ahead, 1, 0)
         ints[3, i] = where
-        mine = table[reader(device), i]
+        mine = slot_of(device, i)
         ints[4, i] = mine
         ints[5, where] = mine
-        ints[6, where] = slot
+        ints[6, where] = found[i]
         floats[0, i] = screen[i, 0].astype(jnp.float32)
         floats[1, where] = screen[i, 1].astype(jnp.float32)
         energy = e_occ[device * own + i]
@@ -516,25 +650,15 @@
     groups = n_occ * n_aux
     depth, held, nvir = integrals.shape
     own = held // n_aux
-    naux = depth * n_aux
     occ, aux = lax.axis_index("occ"), lax.axis_index("aux")
     device = occ * n_aux + aux
 
-    place = jnp.arange(own, dtype=jnp.int32)
-    wanted = jnp.any((partner[:, 1, None] == place) & (screen[:, 1, None] != 0), axis=0)
-    below = place[None, :] < place[:, None]
-    count = jnp.sum(wanted, dtype=jnp.int32)
-    first = jnp.sum(below & wanted[None, :], axis=1, dtype=jnp.int32)
-    rank = jnp.where(wanted, first, count + place - first)
-    order = jnp.sum(jnp.where(rank[None, :] == place[:, None], place[None, :], 0), axis=1)
-    lines = jnp.concatenate([rank, order, count[None]])[None]
-    lines = jnp.pad(lines, ((0, 7), (0, 128 - 2 * own - 1)))
-    table = everyones(lines, n_occ, n_aux)[:, 0, :]
+    table = rankings(partner, screen, n_occ, n_aux)
 
     reader = ((occ + n_occ // 2) % n_occ) * n_aux
     packed = packed_blocks(integrals, reader[None], table, n_aux)
 
-    choices = sorted(set(range(own + 2, 2 * own - 2)) | {2 * own})
+    choices = sorted(set(range(own + 1, 2 * own - 3)) | {2 * own})
     ints, floats, branch = plan(choices, table, partner, screen, e_occ, n_occ, n_aux)
 
     def chosen(total):

time: 701 us -> 666 us (0.950)
  Pallas kernels: 688 us -> 658 us
    pallas_call x1, Pallas kernels: 625 us -> 593 us  [moved(): pl.pallas_call(functools.partial(move_kernel, total, n_occ, n_aux), out_s...]
where the time goes in v1:
time: 666 us; the launch traced here: 665 us
  Pallas kernels  658 us (99%)
    pallas_call x1, Pallas kernels, moved(): pl.pallas_call(functools.partial(move_kernel, total, n_occ, n_aux), out_s...  593 us
    pallas_call x1, Pallas kernels, gradient(): pl.pallas_call(functools.partial(gamma_kernel, own), grid_spec=pltpu.Pref...  28.2 us
    pallas_call x1, Pallas kernels, packed_blocks(): pl.pallas_call(pack_kernel, grid_spec=pltpu.PrefetchScalarGridSpec(num_sc...  20.6 us

profile of v1, /device:TPU:0, one launch (start us, length us, event | category | flops | bytes accessed | tf_op | source)
XLA Modules:
  0.0 664.8 jit_solution(791621841119735366)
XLA Ops:
  0.6 1.3 copy.17.partner
  2.0 1.3 copy.18.screen
  3.3 12.0 %shard_map.77.table = s32[32,1,128]{2,1,0:T(1,128)} custom-call(s32[8,2]{1,0:T(8,128)} %copy.17.partner, s32[8,2]{1,0:T(8,128)} %copy.18.screen), custom_call_target="tpu_custom_call" | custom-call | tf_op jit(solution)/shard_map/pallas_call | solution.py:114
  15.4 4.3 shard_map.78
  20.3 0.0 copy-start
  20.3 20.6 %shard_map.79 = bf16[4,8,512,512]{3,2,1,0:T(8,128)(2,1)} custom-call(s32[1]{0:T(128)} %bitcast.11.base, s32[32,1,128]{2,1,0:T(1,128)} %shard_map.77.table, bf16[512,32,512]{2,1,0:T(8,128)(2,1)} %x.1), custom_call_target="tpu_custom_call" | custom-call | tf_op jit(solution)/shard_map/pallas_call | solution.py:141
  40.9 0.0 copy-done
  40.9 595.1 %conditional.1 = (bf16[9,2048,512]{2,1,0:T(8,128)(2,1)}, f32[8,2048,512]{2,1,0:T(8,128)}, bf16[8,512,512]{2,1,0:T(8,128)(2,1)}, f32[64,512]{1,0:T(8,128)}) conditional(s32[]{:T(128)} %bitcast.10, (f32[512]{0:T(512)S(1)}, s32[7,8]{1,0:T(8,128)}, f32[6,8]{1,0:T(8,128)}, bf16[4,8,512,512]{3,2,1,0:T(8,128)(2,1)}, ...), branch_computations={%region_0.1_spmd, %region_1.2_spmd, %region_2.3_spmd, %region_3.4_... | conditional | bytes 12348 | solution.py:668
  40.9 0.0 copy-start.2
  40.9 0.6 copy-done.2
  41.5 0.9 copy.13.col
  42.3 593.1 %branch_1_fun.1 = (bf16[9,2048,512]{2,1,0:T(8,128)(2,1)}, f32[8,2048,512]{2,1,0:T(8,128)}, bf16[8,2048,512]{2,1,0:T(8,128)(2,1)}, bf16[8,512,512]{2,1,0:T(8,128)...) custom-call(s32[7,8]{1,0:T(8,128)} %get-tuple-element.59.ints, ...), custom_call_target="tpu_custom_call" | custom-call | tf_op jit(solution)/shard_map/cond/branch_1_fun/pallas_call | solution.py:463
  636.0 0.0 copy-start.6
  636.0 28.2 %shard_map.80 = bf16[2048,8,512]{2,1,0:T(8,128)(2,1)} custom-call(s32[7,8]{1,0:T(8,128)} %get-tuple-element.104.at, bf16[9,2048,512]{2,1,0:T(8,128)(2,1)} %get-tuple-element.107.right, bf16[8,512,512]{2,1,0:T(8,128)(2,1)} %get-tuple-element.108.amp, f32[8,2048,512]{2,1,0:T(8,128)} %get-tuple-element.109.begun), custom_call_target="tpu_custom_call" | custom-call | tf_op jit(solution)/shard_map/pallas_call | solution.py:33
  664.2 0.0 copy-done.6
  664.2 0.7 copy.42
Async XLA Ops:
  20.3 20.6 %copy-start = (f32[512]{0:T(512)S(1)}, f32[512]{0:T(512)}, u32[]{:S(2)}) copy-start(f32[512]{0:T(512)} %param.14) | copy-start | bytes 6148
  40.9 0.6 copy-start.2
  636.0 28.2 %copy-start.6 = (f32[64,512]{1,0:T(8,128)S(1)}, f32[64,512]{1,0:T(8,128)}, u32[]{:S(2)}) copy-start(f32[64,512]{1,0:T(8,128)} %get-tuple-element.134) | copy-start | bytes 393220

commit v2 on v1

--- a/solution.py
+++ b/solution.py
@@ -299,8 +299,21 @@
 
         return carry
 
+    def relay():
+        first = cap - spill
+        far_copy(coeff.at[first], first).wait_recv()
+        back_copy().start()
+        cross_copy(first, 0, cap_mate).start()
+        far_copy(fills.at[spill - 1], cap - 1).start()
+
     def near_slot(t, carry):
         transform(1, lent, t)
+        if pooled:
+
+            @pl.when(t == own - 2)
+            def _():
+                relay()
+
         return carry
 
     lax.fori_loop(0, own, send_own, 0)
@@ -322,7 +335,10 @@
 
         lax.fori_loop(0, naux // tile, copy, 0)
         put(stage, fills.at[f])
-        far_copy(fills.at[f], cap - spill + f).start()
+        @pl.when(f < spill - 1)
+        def _():
+            far_copy(fills.at[f], cap - spill + f).start()
+
         return carry
 
     lax.fori_loop(0, spill, fill, 0)
@@ -359,14 +375,13 @@
         return carry
 
     def arrive(u, carry):
-        far_copy(coeff.at[u], u).wait_recv()
+        @pl.when(u != cap - spill if pooled else u >= 0)
+        def _():
+            far_copy(coeff.at[u], u).wait_recv()
+
         if pooled:
 
-            @pl.when(u == cap - spill)
-            def _():
-                back_copy().start()
-
-            @pl.when(u >= cap - spill)
+            @pl.when(u > cap - spill)
             def _():
                 cross_copy(u, jnp.maximum(u - (cap - spill), 0), cap_mate).start()
 

time: 666 us -> 631 us (0.947)
  Pallas kernels: 658 us -> 623 us
    pallas_call x1, Pallas kernels: 593 us -> 558 us  [moved(): pl.pallas_call(functools.partial(move_kernel, total, n_occ, n_aux), out_s...]
where the time goes in v2:
time: 631 us; the launch traced here: 630 us
  Pallas kernels  623 us (99%)
    pallas_call x1, Pallas kernels, moved(): pl.pallas_call(functools.partial(move_kernel, total, n_occ, n_aux), out_s...  558 us
    pallas_call x1, Pallas kernels, gradient(): pl.pallas_call(functools.partial(gamma_kernel, own), grid_spec=pltpu.Pref...  28.2 us
    pallas_call x1, Pallas kernels, packed_blocks(): pl.pallas_call(pack_kernel, grid_spec=pltpu.PrefetchScalarGridSpec(num_sc...  20.6 us

profile of v2, /device:TPU:0, one launch (start us, length us, event | category | flops | bytes accessed | tf_op | source)
XLA Modules:
  0.0 630.1 jit_solution(5089692514233905544)
XLA Ops:
  0.6 1.3 copy.17.partner
  2.0 1.3 copy.18.screen
  3.3 12.0 %shard_map.77.table = s32[32,1,128]{2,1,0:T(1,128)} custom-call(s32[8,2]{1,0:T(8,128)} %copy.17.partner, s32[8,2]{1,0:T(8,128)} %copy.18.screen), custom_call_target="tpu_custom_call" | custom-call | tf_op jit(solution)/shard_map/pallas_call | solution.py:114
  15.4 4.3 shard_map.78
  20.3 0.0 copy-start
  20.3 20.6 %shard_map.79 = bf16[4,8,512,512]{3,2,1,0:T(8,128)(2,1)} custom-call(s32[1]{0:T(128)} %bitcast.11.base, s32[32,1,128]{2,1,0:T(1,128)} %shard_map.77.table, bf16[512,32,512]{2,1,0:T(8,128)(2,1)} %x.1), custom_call_target="tpu_custom_call" | custom-call | tf_op jit(solution)/shard_map/pallas_call | solution.py:141
  40.9 0.0 copy-done
  40.9 560.4 %conditional.1 = (bf16[9,2048,512]{2,1,0:T(8,128)(2,1)}, f32[8,2048,512]{2,1,0:T(8,128)}, bf16[8,512,512]{2,1,0:T(8,128)(2,1)}, f32[64,512]{1,0:T(8,128)}) conditional(s32[]{:T(128)} %bitcast.10, (f32[512]{0:T(512)S(1)}, s32[7,8]{1,0:T(8,128)}, f32[6,8]{1,0:T(8,128)}, bf16[4,8,512,512]{3,2,1,0:T(8,128)(2,1)}, ...), branch_computations={%region_0.1_spmd, %region_1.2_spmd, %region_2.3_spmd, %region_3.4_... | conditional | bytes 12348 | solution.py:683
  40.9 0.0 copy-start.1
  40.9 0.6 copy-done.1
  41.5 0.9 copy.12.col
  42.3 558.2 %branch_0_fun.1 = (bf16[9,2048,512]{2,1,0:T(8,128)(2,1)}, f32[8,2048,512]{2,1,0:T(8,128)}, bf16[8,2048,512]{2,1,0:T(8,128)(2,1)}, bf16[8,512,512]{2,1,0:T(8,128)...) custom-call(s32[7,8]{1,0:T(8,128)} %get-tuple-element.50.ints, ...), custom_call_target="tpu_custom_call" | custom-call | tf_op jit(solution)/shard_map/cond/branch_0_fun/pallas_call | solution.py:478
  601.3 0.0 copy-start.6
  601.3 28.2 %shard_map.80 = bf16[2048,8,512]{2,1,0:T(8,128)(2,1)} custom-call(s32[7,8]{1,0:T(8,128)} %get-tuple-element.104.at, bf16[9,2048,512]{2,1,0:T(8,128)(2,1)} %get-tuple-element.107.right, bf16[8,512,512]{2,1,0:T(8,128)(2,1)} %get-tuple-element.108.amp, f32[8,2048,512]{2,1,0:T(8,128)} %get-tuple-element.109.begun), custom_call_target="tpu_custom_call" | custom-call | tf_op jit(solution)/shard_map/pallas_call | solution.py:33
  629.4 0.0 copy-done.6
  629.4 0.7 copy.42
Async XLA Ops:
  20.3 20.6 %copy-start = (f32[512]{0:T(512)S(1)}, f32[512]{0:T(512)}, u32[]{:S(2)}) copy-start(f32[512]{0:T(512)} %param.14) | copy-start | bytes 6148
  40.9 0.6 copy-start.1
  601.3 28.2 %copy-start.6 = (f32[64,512]{1,0:T(8,128)S(1)}, f32[64,512]{1,0:T(8,128)}, u32[]{:S(2)}) copy-start(f32[64,512]{1,0:T(8,128)} %get-tuple-element.134) | copy-start | bytes 393220
